TPU v7x, 32 devices: a whole 2x2x4 slice. The times are simulated.
32 devices in a mesh: slab: 4 (over y, core), wide: 8 (over z, x).
Axes of the slice: x: 2, y: 2, z: 4, core: 2. Of those that a mesh axis runs over, the one named last changes fastest.
Arguments:
- spectrum: float32 [1152, 32, 128], P('wide', 'slab'), may hold values from 0 to 1
- sea_mask: int32 [32, 128], P('slab'), may hold values 0 or 1
- courant: float32 [32], replicated, may hold values from 0.05 to 0.7
- slot_owner: int32 [1152], replicated, may hold values from 0 to 1151, each once
- coupling: bfloat16 [1152, 1152], replicated, may hold values from -0.1875 to 0.1875
Outputs:
- evolved: float32 [1152, 32, 128], P('wide', 'slab')
Inputs may be any that keep to these rules, and one draw needn't show every extreme that they name: `slot_owner`: each component occurs in exactly one slot; component f * 36 + d has direction d and frequency f. `sea_mask`: 1 marks a sea point.
All inputs are finite; a program needn't handle non-finite values. No bound on the sum of `sea_mask` on one device may be relied on, other than what follows from the above.
Results may differ from a plain program's by a relative error of at most 0.0015.
Values sent between devices are 32-bit elements; how exact they have to be, the bound alone decides.
No kernel may reach another device: no remote copies, remote signals or barrier semaphores. Data moves between devices by JAX's collectives and lax.ppermute only.
A program may use at most 64 MiB of HBM per device.

v0:
```python
import functools
import math

import jax
import jax.numpy as jnp
import numpy as np
from jax import lax
from jax.experimental import pallas as pl
from jax.experimental.pallas import tpu as pltpu
from jax.sharding import PartitionSpec as P


ND = 36
STEPS = 2
LANES = 128
SUBS = 8
SWAP_ORDER = (4, 1, 6, 2, 5, 3, 7)

time_step = 0.5


def extended(cells, sides, width):
    for axis, dim in sides:
        count = lax.axis_size(axis)
        ends = count - 1
        head = lax.slice_in_dim(cells, 0, width, axis=dim)
        tail = lax.slice_in_dim(cells, cells.shape[dim] - width, cells.shape[dim], axis=dim)
        cells = jnp.concatenate(
            [
                lax.ppermute(tail, axis, [(i, (i + 1) % count) for i in range(ends)]),
                cells,
                lax.ppermute(head, axis, [((i + 1) % count, i) for i in range(ends)]),
            ],
            axis=dim,
        )
    return cells


def velocities(slot_owner, courant):
    band_count = courant.shape[0]
    heading = slot_owner % ND
    freq_band = slot_owner // ND
    picked = freq_band[:, None] == jnp.arange(band_count, dtype=jnp.int32)[None, :]
    wave_speed = jnp.sum(jnp.where(picked, courant[None, :], 0.0), axis=1)
    wave_angle = heading.astype(jnp.float32) * (2.0 * math.pi / ND)
    return (wave_speed * jnp.cos(wave_angle), wave_speed * jnp.sin(wave_angle))


def combine_sides(energy, west_side, east_side, south_side, north_side, east_speed, north_speed):
    east_speed = east_speed[:, None, None]
    north_speed = north_speed[:, None, None]
    remain = 1.0 - jnp.abs(east_speed) - jnp.abs(north_speed)
    result = remain * energy + jnp.maximum(east_speed, 0.0) * west_side
    result = result + jnp.maximum(-east_speed, 0.0) * east_side
    result = result + jnp.maximum(north_speed, 0.0) * south_side
    return result + jnp.maximum(-north_speed, 0.0) * north_side


def advect(energy, padded, east_speed, north_speed):
    west_side = jnp.roll(energy, 1, axis=2)
    east_side = jnp.roll(energy, -1, axis=2)
    return combine_sides(
        energy, west_side, east_side, padded[:, :-2, :], padded[:, 2:, :], east_speed, north_speed
    )


def interact(moved, slot_table):
    slot_count = moved.shape[0]
    flattened = moved.reshape(slot_count, -1)
    rounded = flattened.astype(jnp.bfloat16)
    square = (flattened * flattened).astype(jnp.bfloat16)
    gain_term = flattened * jnp.dot(slot_table, rounded, preferred_element_type=jnp.float32)
    loss_term = lax.dot_general(
        slot_table, square, (((0,), (0,)), ((), ())), preferred_element_type=jnp.float32
    )
    updated = jnp.maximum(flattened + time_step * (gain_term - loss_term), 0.0)
    return updated.reshape(moved.shape)


def general_body(spectrum, sea_mask, courant, slot_owner, coupling):
    slot_count = spectrum.shape[0]
    wide_index = lax.axis_index("wide")
    sea_float = sea_mask.astype(jnp.float32)
    slot_table = jnp.take(jnp.take(coupling, slot_owner, axis=0), slot_owner, axis=1)
    energy = spectrum * sea_float[None]
    own_slots = lax.dynamic_slice_in_dim(slot_owner, wide_index * slot_count, slot_count, 0)
    east_speed, north_speed = velocities(own_slots, courant)
    for _ in range(STEPS):
        padded = extended(energy, (("slab", 1),), 1)
        moved = advect(energy, padded, east_speed, north_speed)
        energy = (
            lax.all_to_all(
                interact(
                    lax.all_to_all(moved, "wide", split_axis=1, concat_axis=0, tiled=True),
                    slot_table,
                ),
                "wide",
                split_axis=0,
                concat_axis=1,
                tiled=True,
            )
            * sea_float[None]
        )
    return energy


def ring_order(count):
    return list(range(0, count, 2)) + list(range(1, count, 2))[::-1]


def column_block(device, count):
    half = device // 2
    return jnp.where(device % 2 == 0, half, count - 1 - half)


def trig_table():
    angle = np.arange(ND, dtype=np.float32) * np.float32(2.0 * math.pi / ND)
    table = np.zeros((SUBS, LANES), np.float32)
    table[0, :ND], table[1, :ND] = np.cos(angle), np.sin(angle)
    return table[:2]


def pairs(count, odd, closed=False):
    found = [(i, (i + 1) % count) for i in range(odd, count, 2) if closed or i + 1 < count]
    return found + [(b, a) for a, b in found]


def shares(east, north):
    return (
        1.0 - jnp.abs(east) - jnp.abs(north),
        jnp.maximum(east, 0.0),
        jnp.maximum(-east, 0.0),
        jnp.maximum(north, 0.0),
        jnp.maximum(-north, 0.0),
    )


def swap_lane_blocks(parts, width):
    count = len(parts)
    lane = lax.broadcasted_iota(jnp.int32, parts[0].shape, 1)
    bit = 1
    while bit < count:
        low = (lane & (bit * width)) == 0
        other = lane ^ (bit * width)
        done = list(parts)
        for a in range(count):
            if a & bit:
                continue
            b = a | bit
            crossed = jnp.take_along_axis(jnp.where(low, parts[b], parts[a]), other, axis=1)
            done[a] = jnp.where(low, parts[a], crossed)
            done[b] = jnp.where(low, crossed, parts[b])
        parts = done
        bit *= 2
    return parts


def chunks(count, step):
    return [(c, min(step, count - c)) for c in range(0, count, step)]


def as_column(row):
    size = row.shape[1]
    line = lax.broadcasted_iota(jnp.int32, (size, size), 0)
    lane = lax.broadcasted_iota(jnp.int32, (size, size), 1)
    column = jnp.sum(jnp.where(line == lane, row, 0.0), axis=1, keepdims=True)
    return jnp.broadcast_to(column, (size, LANES))


def speed_lookup(courant, table):
    courant = as_column(courant)
    cosine_of = as_column(table[0:1])
    sine_of = as_column(table[1:2])
    bands = lax.broadcasted_iota(jnp.int32, courant.shape, 0)
    headings = lax.broadcasted_iota(jnp.int32, cosine_of.shape, 0)

    def speeds(component):
        band = component // ND
        heading = component - band * ND
        speed = jnp.sum(jnp.where(bands == band, courant, 0.0), axis=0, keepdims=True)
        cosine = jnp.sum(jnp.where(headings == heading, cosine_of, 0.0), axis=0, keepdims=True)
        sine = jnp.sum(jnp.where(headings == heading, sine_of, 0.0), axis=0, keepdims=True)
        return speed * cosine, speed * sine

    return speeds


def prepare_kernel(x_hbm, mask_hbm, owner_hbm, courant_hbm, table_hbm, a_ref, b_ref, rows_ref, sea_ref, own_ref, mask_ref, owner_ref, courant_ref, table_ref, row_sem, sem):
    slots = a_ref.shape[0]
    me = lax.axis_index("wide")
    even = lax.axis_index("slab") % 2 == 0
    small = [
        pltpu.make_async_copy(source, target, sem.at[k])
        for k, (source, target) in enumerate(
            ((mask_hbm, mask_ref), (owner_hbm, owner_ref), (courant_hbm, courant_ref), (table_hbm, table_ref))
        )
    ]
    order = (0, SUBS - 1) + tuple(range(1, SUBS - 1))
    large = [
        pltpu.make_async_copy(x_hbm.at[:, r, :], rows_ref.at[r, pl.ds(0, slots), :], row_sem.at[r]) for r in order
    ]
    for copy in small + large:
        copy.start()
    for copy in small:
        copy.wait()
    sea = mask_ref[...].astype(jnp.float32)
    sea_ref[...] = sea
    speeds = speed_lookup(courant_ref[...], table_ref[...])
    lanes = lax.broadcasted_iota(jnp.int32, (slots, LANES), 1)
    nth = lax.broadcasted_iota(jnp.int32, (slots, LANES), 0) + me * slots
    own = [jnp.zeros((slots, LANES), jnp.float32) for _ in range(2)]

    for k in range(owner_ref.shape[0]):
        here = lanes + k * LANES == nth
        own = [value + jnp.where(here, one, 0.0) for value, one in zip(own, speeds(owner_ref[k : k + 1, :]))]
    east, north = (jnp.sum(value, axis=1, keepdims=True) for value in own)
    for n, share in enumerate(shares(east, north)):
        own_ref[n, :slots, :] = jnp.broadcast_to(share, (slots, LANES))

    for copy in large:
        copy.wait()
    head = rows_ref[0, :slots, :] * sea[0:1]
    tail = rows_ref[SUBS - 1, :slots, :] * sea[SUBS - 1 : SUBS]
    a_ref[...] = jnp.where(even, tail, head)
    b_ref[...] = jnp.where(even, head, tail)


def by_device(parts, me):
    bit = 1
    while bit < len(parts):
        flip = (me & bit) != 0
        parts = [jnp.where(flip, parts[k ^ bit], parts[k]) for k in range(len(parts))]
        bit *= 2
    return parts


def spread_kernel(ring, cols, x_ref, sea_ref, own_ref, out_ref):
    slots = x_ref.shape[1] - SUBS
    sea = [jnp.broadcast_to(sea_ref[r : r + 1, :], (SUBS, LANES)) for r in range(SUBS)]
    for base in range(0, slots, SUBS):
        here = slice(base, base + SUBS)
        remain, west_in, east_in, south_in, north_in = (own_ref[k, here, :] for k in range(5))
        rows = [x_ref[r, here, :] * sea[r] for r in range(SUBS)]
        moved = []
        for r in range(SUBS):
            value = remain * rows[r] + west_in * pltpu.roll(rows[r], 1, 1)
            value = value + east_in * pltpu.roll(rows[r], LANES - 1, 1)
            if r > 0:
                value = value + south_in * rows[r - 1]
            if r < SUBS - 1:
                value = value + north_in * rows[r + 1]
            moved.append(value)
        for device, block in zip(ring, swap_lane_blocks(moved, cols)):
            out_ref[device, here, :] = block


def border_kernel(ring, cols, x_ref, a_ref, b_ref, own_ref, *outs):
    slots = a_ref.shape[0]
    me = lax.axis_index("wide")
    even = lax.axis_index("slab") % 2 == 0
    lane = lax.broadcasted_iota(jnp.int32, (SUBS, LANES), 1)
    border = (lane < cols) | (lane >= LANES - cols)
    for base in range(0, slots, SUBS):
        here = slice(base, base + SUBS)
        a, b = a_ref[here, :], b_ref[here, :]
        south = own_ref[3, here, :] * jnp.where(even, b, a)
        north = pltpu.roll(own_ref[4, here, :] * jnp.where(even, a, b), LANES - cols, 1)
        blocks = [None] * len(ring)
        for n, device in enumerate(ring):
            both = jnp.where(lane // cols == n, south, north)
            both = pltpu.roll(both, LANES - n * cols, 1) if n else both
            blocks[device] = x_ref[device, here, :] + jnp.where(border, both, 0.0)
        blocks = by_device(blocks, me)
        for k, out in zip((0,) + SWAP_ORDER, outs):
            out[here, :] = blocks[k]


def gather_kernel(ring, cols, *refs):
    parts, out_hbm, rows_ref, sem = refs[: len(ring)], *refs[len(ring) :]
    slots = parts[0].shape[0]
    me = lax.axis_index("wide")
    by_swap = dict(zip((0,) + SWAP_ORDER, parts))
    third = slots // 3
    copies = []
    for base in range(0, slots, SUBS):
        here = slice(base, base + SUBS)
        blocks = by_device([by_swap[k][here, :] for k in range(len(ring))], me)
        for r, row in enumerate(swap_lane_blocks([blocks[device] for device in ring], cols)):
            rows_ref[r, here, :] = row
        if (base + SUBS) % third == 0:
            done = slice(base + SUBS - third, base + SUBS)
            for r in range(SUBS):
                copies.append(
                    pltpu.make_async_copy(rows_ref.at[r, done, :], out_hbm.at[done, r, :], sem.at[len(copies)])
                )
                copies[-1].start()
    for copy in copies:
        copy.wait()


ROWS_AT_ONCE = 16
EARLY = 5
LATE = 2


def each_row(swaps, slots, owner_ref, load, store):
    me = lax.axis_index("wide")
    for k in swaps:
        first = (me ^ k) * slots

        def some(g, carry, k=k, first=first):
            for m in range(3):
                base = pl.multiple_of((g * 3 + m) * ROWS_AT_ONCE, ROWS_AT_ONCE)
                places = [(base + n, owner_ref[first + base + n]) for n in range(ROWS_AT_ONCE)]
                values = [load(k, *place) for place in places]
                for place, value in zip(places, values):
                    store(k, *place, value)
            return carry

        lax.fori_loop(0, slots // ROWS_AT_ONCE // 3, some, 0)


def to_smem(source, target, sem):
    copy = pltpu.make_async_copy(source, target, sem)
    copy.start()
    copy.wait()


def place_rows(swaps, parts, rows_ref, owner_ref):
    by_swap = dict(zip(swaps, parts))

    def store(k, row, component, value):
        rows_ref[pl.ds(component, 1), :] = value

    each_row(swaps, parts[0].shape[0], owner_ref, lambda k, row, _: by_swap[k][pl.ds(row, 1), :], store)


def place_kernel(wide, cols, owner_hbm, courant_hbm, table_hbm, coupling_hbm, sea_ref, *refs):
    parts, (rows_ref, block_ref, coupling_ref, share_ref, owner_ref, courant_ref, table_ref, sem) = refs[:EARLY], refs[EARLY:]
    copies = [
        pltpu.make_async_copy(source, target, sem.at[k])
        for k, (source, target) in enumerate(
            (
                (owner_hbm, owner_ref),
                (courant_hbm, courant_ref),
                (table_hbm, table_ref),
                (coupling_hbm, coupling_ref),
            )
        )
    ]
    for copy in copies:
        copy.start()
    me = lax.axis_index("wide")
    sea = sea_ref[...]
    points = SUBS * cols
    line = lax.broadcasted_iota(jnp.int32, (points, LANES), 0)
    lane = lax.broadcasted_iota(jnp.int32, (points, LANES), 1)
    spread = jnp.concatenate([jnp.broadcast_to(sea[r : r + 1], (cols, LANES)) for r in range(SUBS)], axis=0)
    start = column_block(me, wide) * cols
    mine = jnp.sum(jnp.where(lane == line % cols + start, spread, 0.0), axis=1, keepdims=True)
    block_ref[...] = jnp.broadcast_to(mine, (points, LANES))
    for copy in copies[:-1]:
        copy.wait()
    place_rows(((0,) + SWAP_ORDER)[:EARLY], parts, rows_ref, owner_ref)
    speeds = speed_lookup(courant_ref[...], table_ref[...])
    row = lax.broadcasted_iota(jnp.int32, (1, LANES), 1)
    for c in range(0, share_ref.shape[1], LANES):
        for n, share in enumerate(shares(*speeds(row + c))):
            share_ref[n : n + 1, c : c + LANES] = share
    copies[-1].wait()


def place_more_kernel(held_ref, owner_hbm, *refs):
    parts, (rows_ref, owner_ref, sem) = refs[:LATE], refs[LATE:]
    to_smem(owner_hbm, owner_ref, sem)
    place_rows(SWAP_ORDER[EARLY - 1 : EARLY - 1 + LATE], parts, rows_ref, owner_ref)


def contract(moved_ref, rounded_ref, square_ref, table_ref, sea, store):
    count = moved_ref.shape[1]
    for c, step in chunks(count, 2 * LANES):
        gain = lax.dot_general(
            rounded_ref[...],
            table_ref[c : c + step, :],
            (((1,), (1,)), ((), ())),
            preferred_element_type=jnp.float32,
        )
        loss = jnp.dot(square_ref[...], table_ref[:, c : c + step], preferred_element_type=jnp.float32)
        for n in range(0, step, LANES):
            moved = moved_ref[:, c + n : c + n + LANES]
            value = moved + time_step * (moved * gain[:, n : n + LANES] - loss[:, n : n + LANES])
            store(c + n, jnp.maximum(value, 0.0) * sea)


def first_kernel(wide, cols, held_ref, owner_ref, table_ref, sea_ref, *refs):
    late = wide - EARLY - LATE
    parts, (rows_ref, out_ref, a_ref, b_ref, c_ref, d_ref) = refs[:late], refs[late : late + 6]
    moved_ref, rounded_ref, square_ref, value_ref, owner_smem, sem = refs[late + 6 :]
    points, count = out_ref.shape
    row_even = lax.axis_index("slab") % 2 == 0
    col_even = column_block(lax.axis_index("wide"), wide) % 2 == 0
    to_smem(owner_ref, owner_smem, sem)
    place_rows(SWAP_ORDER[EARLY + LATE - 1 :], parts, rows_ref, owner_smem)
    for c in range(0, count, LANES):
        there = slice(c, c + LANES)
        moved = rows_ref[there, :].T
        moved_ref[:, there] = moved
        rounded_ref[:, there] = moved.astype(jnp.bfloat16)
        square_ref[:, there] = (moved * moved).astype(jnp.bfloat16)

    def store(c, value):
        there = slice(c, c + LANES)
        out_ref[:, there] = value
        head, tail = value[:cols], value[points - cols :]
        a_ref[:, there] = jnp.where(row_even, tail, head)
        b_ref[:, there] = jnp.where(row_even, head, tail)
        value_ref[...] = value
        west = value_ref[pl.ds(0, points // cols, stride=cols), :]
        east = value_ref[pl.ds(cols - 1, points // cols, stride=cols), :]
        c_ref[:, there] = jnp.where(col_even, east, west)
        d_ref[:, there] = jnp.where(col_even, west, east)

    contract(moved_ref, rounded_ref, square_ref, table_ref, sea_ref[...], store)


def second_kernel(wide, cols, x_ref, a_ref, b_ref, c_ref, d_ref, share_ref, table_ref, sea_ref, owner_ref, *refs):
    outs, (moved_ref, rounded_ref, square_ref, value_ref, owner_smem, sem) = refs[:wide], refs[wide:]
    copy = pltpu.make_async_copy(owner_ref, owner_smem, sem)
    copy.start()
    points, count = x_ref.shape
    row_even = lax.axis_index("slab") % 2 == 0
    col_even = column_block(lax.axis_index("wide"), wide) % 2 == 0
    line = lax.broadcasted_iota(jnp.int32, (points, LANES), 0) % cols
    for c in range(0, count, LANES):
        there = slice(c, c + LANES)
        here = x_ref[:, there]
        share = [share_ref[k : k + 1, there] for k in range(5)]
        a, b, side_c, side_d = a_ref[:, there], b_ref[:, there], c_ref[:, there], d_ref[:, there]

        def along(edge):
            return jnp.concatenate(
                [jnp.broadcast_to(edge[r : r + 1], (cols, LANES)) for r in range(points // cols)], axis=0
            )

        west_edge = along(jnp.where(col_even, side_d, side_c))
        east_edge = along(jnp.where(col_even, side_c, side_d))
        west = jnp.where(line == 0, west_edge, pltpu.roll(here, 1, 0))
        east = jnp.where(line == cols - 1, east_edge, pltpu.roll(here, points - 1, 0))
        south = jnp.concatenate([jnp.where(row_even, b, a), here[: points - cols]], axis=0)
        north = jnp.concatenate([here[cols:], jnp.where(row_even, a, b)], axis=0)
        moved = share[0] * here + share[1] * west
        moved = moved + share[2] * east
        moved = moved + share[3] * south
        moved = moved + share[4] * north
        moved_ref[:, there] = moved
        rounded_ref[:, there] = moved.astype(jnp.bfloat16)
        square_ref[:, there] = (moved * moved).astype(jnp.bfloat16)

    def store(c, value):
        value_ref[c : c + LANES, :] = value.T

    contract(moved_ref, rounded_ref, square_ref, table_ref, sea_ref[...], store)
    by_swap = dict(zip((0,) + SWAP_ORDER, outs))

    def put(k, row, component, value):
        by_swap[k][pl.ds(row, 1), :] = value

    copy.wait()
    each_row(
        (0,) + SWAP_ORDER, count // wide, owner_smem, lambda k, _, component: value_ref[pl.ds(component, 1), :], put
    )


def block_body(spectrum, sea_mask, courant, slot_owner, coupling):
    slots, rows, lons = spectrum.shape
    wide, slabs = lax.axis_size("wide"), lax.axis_size("slab")
    count = slots * wide
    cols = lons // wide
    points = rows * cols
    ring = ring_order(wide)
    vmem = pl.BlockSpec(memory_space=pltpu.VMEM)
    in_hbm = pl.BlockSpec(memory_space=pltpu.HBM)
    f32, bf16 = jnp.float32, jnp.bfloat16
    shape = jax.ShapeDtypeStruct

    def call(kernel, outs, ins, scratch=(), flops=0, on_chip_result=True, aliases={}):
        made = pl.pallas_call(
            kernel,
            out_shape=jax.tree.map(lambda out: pltpu.VMEM(out.shape, out.dtype), outs) if on_chip_result else outs,
            in_specs=ins,
            out_specs=jax.tree.map(lambda _: vmem if on_chip_result else in_hbm, outs),
            scratch_shapes=scratch,
            input_output_aliases=aliases,
            compiler_params=pltpu.CompilerParams(vmem_limit_bytes=24 << 20),
            cost_estimate=pl.CostEstimate(flops=flops, transcendentals=0, bytes_accessed=0),
        )

        def on_chip(*given):
            return made(
                *(
                    pltpu.with_memory_space_constraint(one, spec.memory_space)
                    for one, spec in zip(given, ins)
                )
            )

        return on_chip

    owners = slot_owner.reshape(count // LANES, LANES)
    edge = shape((slots, LANES), f32)
    trig = trig_table()
    send_a, send_b, lines, sea, own = call(
        prepare_kernel,
        (
            edge,
            edge,
            shape((rows, slots + SUBS, LANES), f32),
            shape((rows, LANES), f32),
            shape((5, slots + SUBS, LANES), f32),
        ),
        [in_hbm] * 5,
        (
            pltpu.VMEM(sea_mask.shape, jnp.int32),
            pltpu.VMEM(owners.shape, jnp.int32),
            pltpu.VMEM((1,) + courant.shape, f32),
            pltpu.VMEM(trig.shape, f32),
            pltpu.SemaphoreType.DMA((rows,)),
            pltpu.SemaphoreType.DMA((4,)),
        ),
    )(spectrum, sea_mask, owners, courant[None, :], jnp.asarray(trig))

    def swap_rows(a, b):
        return lax.ppermute(a, "slab", pairs(slabs, 0)), lax.ppermute(b, "slab", pairs(slabs, 1))

    def swap_cols(c, d):
        def along(odd):
            return [(ring[i], ring[j]) for i, j in pairs(wide, odd, closed=True)]

        return lax.ppermute(c, "wide", along(0)), lax.ppermute(d, "wide", along(1))

    def swap_blocks(blocks):
        swaps = [
            lax.ppermute(block, "wide", [(w, w ^ k) for w in range(wide)])
            for k, block in zip(SWAP_ORDER, blocks[1:])
        ]
        return [blocks[0]] + swaps

    near = swap_rows(send_a, send_b)
    inner = call(
        functools.partial(spread_kernel, ring, cols), shape((wide, slots + SUBS, LANES), f32), [vmem] * 3, flops=10**9
    )(lines, sea, own)
    blocks = call(functools.partial(border_kernel, ring, cols), (edge,) * wide, [vmem] * 4)(
        inner, *near, own
    )
    scratch = (
        pltpu.VMEM((points, count), f32),
        pltpu.VMEM((points, count), bf16),
        pltpu.VMEM((points, count), bf16),
    )
    smem_owners = pltpu.SMEM(slot_owner.shape, jnp.int32)
    arrived = swap_blocks(blocks)
    held, sea_block, table, share = call(
        functools.partial(place_kernel, wide, cols),
        (
            shape((count, points), f32),
            shape((points, LANES), f32),
            shape((count, count), bf16),
            shape((SUBS, count), f32),
        ),
        [in_hbm] * 4 + [vmem] * (1 + EARLY),
        (
            smem_owners,
            pltpu.VMEM((1,) + courant.shape, f32),
            pltpu.VMEM(trig.shape, f32),
            pltpu.SemaphoreType.DMA((4,)),
        ),
        flops=10**9,
    )(slot_owner, courant[None, :], jnp.asarray(trig), coupling, sea, *arrived[:EARLY])
    held = call(
        place_more_kernel,
        shape((count, points), f32),
        [vmem, in_hbm] + [vmem] * LATE,
        (smem_owners, pltpu.SemaphoreType.DMA(())),
        flops=10**9,
        aliases={0: 0},
    )(held, slot_owner, *arrived[EARLY : EARLY + LATE])
    held, energy, send_a, send_b, send_c, send_d = call(
        functools.partial(first_kernel, wide, cols),
        (shape((count, points), f32),)
        + (shape((points, count), f32),)
        + (shape((cols, count), f32),) * 2
        + (shape((rows, count), f32),) * 2,
        [vmem, in_hbm, vmem] + [vmem] * (1 + wide - EARLY - LATE),
        scratch + (pltpu.VMEM((points, LANES), f32), smem_owners, pltpu.SemaphoreType.DMA(())),
        flops=4 * points * count**2,
        aliases={0: 0},
    )(held, slot_owner, table, sea_block, *arrived[EARLY + LATE :])
    sides = swap_cols(send_c, send_d)
    halos = swap_rows(send_a, send_b) + sides
    updated = call(
        functools.partial(second_kernel, wide, cols),
        (edge,) * wide,
        [vmem] * 8 + [in_hbm],
        scratch + (pltpu.VMEM((count, points), f32), smem_owners, pltpu.SemaphoreType.DMA(())),
        flops=4 * points * count**2,
    )(energy, *halos, share, table, sea_block, slot_owner)
    return call(
        functools.partial(gather_kernel, ring, cols),
        shape((slots, rows, lons), f32),
        [vmem] * wide,
        (pltpu.VMEM((rows, slots + SUBS, LANES), f32), pltpu.SemaphoreType.DMA((3 * rows,))),
        on_chip_result=False,
    )(*swap_blocks(updated))


def solution(mesh):
    wide = mesh.shape["wide"]

    def body(spectrum, *rest):
        slots, rows, lons = spectrum.shape
        fits = rows == SUBS and lons == LANES and wide == SUBS and slots % (3 * ROWS_AT_ONCE) == 0
        fits = fits and (slots * wide) % LANES == 0
        return (block_body if fits else general_body)(spectrum, *rest)

    return jax.shard_map(
        body,
        mesh=mesh,
        in_specs=(P("wide", "slab", None), P("slab", None), P(), P(), P()),
        out_specs=P("wide", "slab", None),
        check_vma=False,
    )
```

profile of v0, /device:TPU:0, one launch (start us, length us, event | category | flops | bytes accessed | tf_op | source)
XLA Modules:
  0.0 56.4 jit_solution(6979256738504355852)
XLA Ops:
  0.0 1.6 %shard_map.64 = (f32[144,128]{1,0:T(8,128)S(1)}, f32[144,128]{1,0:T(8,128)S(1)}, f32[8,152,128]{2,1,0:T(8,128)S(1)}, f32[8,128]{1,0:T(8,128)S(1)}, f32[5,152,128]{2,1,0:T(8,128)S(1)}) custom-call(f32[144,8,128]{2,1,0:T(8,128)} %x_hbm.1, s32[8,128]{1,0:T(8,128)} %mask_hbm.1, s32[9,128]{1,0:T(8,128)} %bitcast.2, f32[1,32]{1,0:T(1,128)} %bitcast.3, ...), custom_call_target="tpu_custom_call" | custom-call | tf_op jit(solution)/shard_map/pallas_call | solution.py:499
  1.6 0.6 collective-permute-start
  2.2 0.7 %collective-permute-start.1 = (f32[144,128]{1,0:T(8,128)S(1)}, f32[144,128]{1,0:T(8,128)S(1)}, u32[]{:S(2)}, u32[]{:S(2)}) collective-permute-start(f32[144,128]{1,0:T(8,128)S(1)} %get-tuple-element.39), channel_id=1, source_target_pairs={{8,16},{16,8},{9,17},{17,9},{10,18},{18,10},{11,19},{19,11},{12,20... | collective-permute-start | bytes 221192 | tf_op jit(solution)/shard_map/ppermute | solution.py:532
  2.8 3.1 %shard_map.65.x_ref = f32[8,152,128]{2,1,0:T(8,128)S(1)} custom-call(f32[8,152,128]{2,1,0:T(8,128)S(1)} %get-tuple-element.36.x_ref, f32[8,128]{1,0:T(8,128)S(1)} %get-tuple-element.35.sea_ref, f32[5,152,128]{2,1,0:T(8,128)S(1)} %get-tuple-element.37.own_ref), custom_call_target="tpu_custom_call" | custom-call | flops 1000000000 | tf_op jit(solution)/shard_map/pallas_call | solution.py:499
  6.3 3.7 %collective-permute-start.2 = (f32[144,128]{1,0:T(8,128)S(1)}, f32[144,128]{1,0:T(8,128)S(1)}, u32[]{:S(2)}, u32[]{:S(2)}) collective-permute-start(f32[144,128]{1,0:T(8,128)S(1)} %get-tuple-element.41), channel_id=1, source_target_pairs={{0,4},{1,5},{2,6},{3,7},{4,0},{5,1},{6,2},{7,3},{8,12},{9,13},{10,... | collective-permute-start | bytes 221192 | tf_op jit(solution)/shard_map/ppermute | solution.py:542
  9.9 1.5 %collective-permute-start.3 = (f32[144,128]{1,0:T(8,128)S(1)}, f32[144,128]{1,0:T(8,128)S(1)}, u32[]{:S(2)}, u32[]{:S(2)}) collective-permute-start(f32[144,128]{1,0:T(8,128)S(1)} %get-tuple-element.42), channel_id=1, source_target_pairs={{0,1},{1,0},{2,3},{3,2},{4,5},{5,4},{6,7},{7,6},{8,9},{9,8},{10,11... | collective-permute-start | bytes 221192 | tf_op jit(solution)/shard_map/ppermute | solution.py:542
  11.4 1.3 %collective-permute-start.4 = (f32[144,128]{1,0:T(8,128)S(1)}, f32[144,128]{1,0:T(8,128)S(1)}, u32[]{:S(2)}, u32[]{:S(2)}) collective-permute-start(f32[144,128]{1,0:T(8,128)S(1)} %get-tuple-element.43), channel_id=1, source_target_pairs={{0,6},{1,7},{2,4},{3,5},{4,2},{5,3},{6,0},{7,1},{8,14},{9,15},{10,... | collective-permute-start | bytes 221192 | tf_op jit(solution)/shard_map/ppermute | solution.py:542
  13.0 2.8 %collective-permute-start.6 = (f32[144,128]{1,0:T(8,128)S(1)}, f32[144,128]{1,0:T(8,128)S(1)}, u32[]{:S(2)}, u32[]{:S(2)}) collective-permute-start(f32[144,128]{1,0:T(8,128)S(1)} %get-tuple-element.46), channel_id=1, source_target_pairs={{0,5},{1,4},{2,7},{3,6},{4,1},{5,0},{6,3},{7,2},{8,13},{9,12},{10,... | collective-permute-start | bytes 221192 | tf_op jit(solution)/shard_map/ppermute | solution.py:542
  15.8 1.6 %collective-permute-start.7 = (f32[144,128]{1,0:T(8,128)S(1)}, f32[144,128]{1,0:T(8,128)S(1)}, u32[]{:S(2)}, u32[]{:S(2)}) collective-permute-start(f32[144,128]{1,0:T(8,128)S(1)} %get-tuple-element.47), channel_id=1, source_target_pairs={{0,3},{1,2},{2,1},{3,0},{4,7},{5,6},{6,5},{7,4},{8,11},{9,10},{10,... | collective-permute-start | bytes 221192 | tf_op jit(solution)/shard_map/ppermute | solution.py:542
  17.4 0.9 %collective-permute-start.8 = (f32[144,128]{1,0:T(8,128)S(1)}, f32[144,128]{1,0:T(8,128)S(1)}, u32[]{:S(2)}, u32[]{:S(2)}) collective-permute-start(f32[144,128]{1,0:T(8,128)S(1)} %get-tuple-element.50), channel_id=1, source_target_pairs={{0,7},{1,6},{2,5},{3,4},{4,3},{5,2},{6,1},{7,0},{8,15},{9,14},{10,... | collective-permute-start | bytes 221192 | tf_op jit(solution)/shard_map/ppermute | solution.py:542
  18.3 0.8 %collective-permute-done.5.refs_4_ = f32[144,128]{1,0:T(8,128)S(1)} collective-permute-done((f32[144,128]{1,0:T(8,128)S(1)}, f32[144,128]{1,0:T(8,128)S(1)}, u32[]{:S(2)}, u32[]{:S(2)}) %collective-permute-start.5) | collective-permute-done | bytes 73760 | tf_op jit(solution)/shard_map/ppermute | solution.py:542
  19.0 1.9 %shard_map.67 = (f32[1152,128]{1,0:T(8,128)S(1)}, f32[128,128]{1,0:T(8,128)S(1)}, bf16[1152,1152]{1,0:T(8,128)(2,1)S(1)}, f32[8,1152]{1,0:T(8,128)S(1)}) custom-call(s32[1152]{0:T(1024)} %owner_ref.3, f32[1,32]{1,0:T(1,128)} %bitcast.4, f32[2,128]{1,0:T(2,128)} %constant.2.clone.table_hbm, bf16[1152,1152]{1,0:T(8,128)(2,1)} %coupling_hbm.1, ...), custom_call_target="tpu_custom_call" | custom-call | flops 1000000000 | tf_op jit(solution)/shard_map/pallas_call | solution.py:499
  20.9 1.6 %collective-permute-done.6.refs_0_ = f32[144,128]{1,0:T(8,128)S(1)} collective-permute-done((f32[144,128]{1,0:T(8,128)S(1)}, f32[144,128]{1,0:T(8,128)S(1)}, u32[]{:S(2)}, u32[]{:S(2)}) %collective-permute-start.6) | collective-permute-done | bytes 73760 | tf_op jit(solution)/shard_map/ppermute | solution.py:542
  22.5 1.1 %shard_map.68.held_ref = f32[1152,128]{1,0:T(8,128)S(1)} custom-call(f32[1152,128]{1,0:T(8,128)S(1)} %get-tuple-element.45.held_ref, s32[1152]{0:T(1024)} %owner_ref.3, f32[144,128]{1,0:T(8,128)S(1)} %collective-permute-done.6.refs_0_, f32[144,128]{1,0:T(8,128)S(1)} %collective-permute-done.7.refs_1_), custom_call_target="tpu_custom_call", output_to_operand_aliasing={{}: (0, {})} | custom-call | flops 1000000000 | tf_op jit(solution)/shard_map/pallas_call | solution.py:499
  23.6 1.5 %collective-permute-done.8.refs_0_ = f32[144,128]{1,0:T(8,128)S(1)} collective-permute-done((f32[144,128]{1,0:T(8,128)S(1)}, f32[144,128]{1,0:T(8,128)S(1)}, u32[]{:S(2)}, u32[]{:S(2)}) %collective-permute-start.8) | collective-permute-done | bytes 73760 | tf_op jit(solution)/shard_map/ppermute | solution.py:542
  25.1 2.4 %shard_map.69 = (f32[1152,128]{1,0:T(8,128)S(1)}, f32[128,1152]{1,0:T(8,128)S(1)}, f32[16,1152]{1,0:T(8,128)S(1)}, f32[16,1152]{1,0:T(8,128)S(1)}, f32[8,1152]{1,0:T(8,128)S(1)}, /*index=5*/f32[8,1152]{1,0:T(8,128)S(1)}) custom-call(f32[1152,128]{1,0:T(8,128)S(1)} %shard_map.68.held_ref, s32[1152]{0:T(1024)} %owner_ref.3, ...), custom_call_target="tpu_custom_call", output_to_operand_aliasing={{0}: (0, {})} | custom-call | flops 679477248 | tf_op jit(solution)/shard_map/pallas_call | solution.py:499
  27.5 0.4 collective-permute-start.9
  27.9 0.7 %collective-permute-start.10 = (f32[16,1152]{1,0:T(8,128)S(1)}, f32[16,1152]{1,0:T(8,128)S(1)}, u32[]{:S(2)}, u32[]{:S(2)}) collective-permute-start(f32[16,1152]{1,0:T(8,128)S(1)} %get-tuple-element.53), channel_id=1, source_target_pairs={{8,16},{16,8},{9,17},{17,9},{10,18},{18,10},{11,19},{19,11},{12,20... | collective-permute-start | bytes 221192 | tf_op jit(solution)/shard_map/ppermute | solution.py:532
  28.6 1.0 %collective-permute-start.11 = (f32[8,1152]{1,0:T(8,128)S(1)}, f32[8,1152]{1,0:T(8,128)S(1)}, u32[]{:S(2)}, u32[]{:S(2)}) collective-permute-start(f32[8,1152]{1,0:T(8,128)S(1)} %get-tuple-element.54), channel_id=1, source_target_pairs={{0,2},{4,6},{7,5},{3,1},{2,0},{6,4},{5,7},{1,3},{8,10},{12,14},{15... | collective-permute-start | bytes 110600 | tf_op jit(solution)/shard_map/ppermute | solution.py:538
  29.6 0.9 %collective-permute-start.12 = (f32[8,1152]{1,0:T(8,128)S(1)}, f32[8,1152]{1,0:T(8,128)S(1)}, u32[]{:S(2)}, u32[]{:S(2)}) collective-permute-start(f32[8,1152]{1,0:T(8,128)S(1)} %get-tuple-element.55), channel_id=1, source_target_pairs={{2,4},{6,7},{5,3},{1,0},{4,2},{7,6},{3,5},{0,1},{10,12},{14,15},{1... | collective-permute-start | bytes 110600 | tf_op jit(solution)/shard_map/ppermute | solution.py:538
  30.5 2.1 %collective-permute-done.11.c_ref = f32[8,1152]{1,0:T(8,128)S(1)} collective-permute-done((f32[8,1152]{1,0:T(8,128)S(1)}, f32[8,1152]{1,0:T(8,128)S(1)}, u32[]{:S(2)}, u32[]{:S(2)}) %collective-permute-start.11) | collective-permute-done | bytes 36896 | tf_op jit(solution)/shard_map/ppermute | solution.py:538
  32.6 1.0 %collective-permute-done.12.d_ref = f32[8,1152]{1,0:T(8,128)S(1)} collective-permute-done((f32[8,1152]{1,0:T(8,128)S(1)}, f32[8,1152]{1,0:T(8,128)S(1)}, u32[]{:S(2)}, u32[]{:S(2)}) %collective-permute-start.12) | collective-permute-done | bytes 36896 | tf_op jit(solution)/shard_map/ppermute | solution.py:538
  33.6 2.7 %shard_map.70 = (f32[144,128]{1,0:T(8,128)S(1)}, f32[144,128]{1,0:T(8,128)S(1)}, f32[144,128]{1,0:T(8,128)S(1)}, f32[144,128]{1,0:T(8,128)S(1)}, f32[144,128]{1,...) custom-call(f32[128,1152]{1,0:T(8,128)S(1)} %get-tuple-element.51.x_ref, ...), custom_call_target="tpu_custom_call" | custom-call | flops 679477248 | tf_op jit(solution)/shard_map/pallas_call | solution.py:499
  36.3 3.2 %collective-permute-start.13 = (f32[144,128]{1,0:T(8,128)S(1)}, f32[144,128]{1,0:T(8,128)S(1)}, u32[]{:S(2)}, u32[]{:S(2)}) collective-permute-start(f32[144,128]{1,0:T(8,128)S(1)} %get-tuple-element.58), channel_id=1, source_target_pairs={{0,4},{1,5},{2,6},{3,7},{4,0},{5,1},{6,2},{7,3},{8,12},{9,13},{10,... | collective-permute-start | bytes 221192 | tf_op jit(solution)/shard_map/ppermute | solution.py:542
  39.5 0.9 %collective-permute-start.15 = (f32[144,128]{1,0:T(8,128)S(1)}, f32[144,128]{1,0:T(8,128)S(1)}, u32[]{:S(2)}, u32[]{:S(2)}) collective-permute-start(f32[144,128]{1,0:T(8,128)S(1)} %get-tuple-element.60), channel_id=1, source_target_pairs={{0,6},{1,7},{2,4},{3,5},{4,2},{5,3},{6,0},{7,1},{8,14},{9,15},{10,... | collective-permute-start | bytes 221192 | tf_op jit(solution)/shard_map/ppermute | solution.py:542
  40.4 0.5 collective-permute-start.16
  40.9 4.5 %collective-permute-start.17 = (f32[144,128]{1,0:T(8,128)S(1)}, f32[144,128]{1,0:T(8,128)S(1)}, u32[]{:S(2)}, u32[]{:S(2)}) collective-permute-start(f32[144,128]{1,0:T(8,128)S(1)} %get-tuple-element.62), channel_id=1, source_target_pairs={{0,5},{1,4},{2,7},{3,6},{4,1},{5,0},{6,3},{7,2},{8,13},{9,12},{10,... | collective-permute-start | bytes 221192 | tf_op jit(solution)/shard_map/ppermute | solution.py:542
  45.4 2.0 %collective-permute-start.19 = (f32[144,128]{1,0:T(8,128)S(1)}, f32[144,128]{1,0:T(8,128)S(1)}, u32[]{:S(2)}, u32[]{:S(2)}) collective-permute-start(f32[144,128]{1,0:T(8,128)S(1)} %get-tuple-element.64), channel_id=1, source_target_pairs={{0,7},{1,6},{2,5},{3,4},{4,3},{5,2},{6,1},{7,0},{8,15},{9,14},{10,... | collective-permute-start | bytes 221192 | tf_op jit(solution)/shard_map/ppermute | solution.py:542
  47.4 2.3 %collective-permute-done.17.refs_5_ = f32[144,128]{1,0:T(8,128)S(1)} collective-permute-done((f32[144,128]{1,0:T(8,128)S(1)}, f32[144,128]{1,0:T(8,128)S(1)}, u32[]{:S(2)}, u32[]{:S(2)}) %collective-permute-start.17) | collective-permute-done | bytes 73760 | tf_op jit(solution)/shard_map/ppermute | solution.py:542
  49.6 2.0 %collective-permute-done.18.refs_6_ = f32[144,128]{1,0:T(8,128)S(1)} collective-permute-done((f32[144,128]{1,0:T(8,128)S(1)}, f32[144,128]{1,0:T(8,128)S(1)}, u32[]{:S(2)}, u32[]{:S(2)}) %collective-permute-start.18) | collective-permute-done | bytes 73760 | tf_op jit(solution)/shard_map/ppermute | solution.py:542
  51.7 2.5 %collective-permute-done.19.refs_7_ = f32[144,128]{1,0:T(8,128)S(1)} collective-permute-done((f32[144,128]{1,0:T(8,128)S(1)}, f32[144,128]{1,0:T(8,128)S(1)}, u32[]{:S(2)}, u32[]{:S(2)}) %collective-permute-start.19) | collective-permute-done | bytes 73760 | tf_op jit(solution)/shard_map/ppermute | solution.py:542
  54.2 2.2 %shard_map.71 = f32[144,8,128]{2,1,0:T(8,128)} custom-call(f32[144,128]{1,0:T(8,128)S(1)} %get-tuple-element.57.refs_0_, f32[144,128]{1,0:T(8,128)S(1)} %collective-permute-done.13.refs_1_, f32[144,128]{1,0:T(8,128)S(1)} %collective-permute-done.14.refs_2_, f32[144,128]{1,0:T(8,128)S(1)} %collective-permute-done.15.refs_3_, ...), custom_call_target="tpu_custom_call" | custom-call | tf_op jit(solution)/shard_map/pallas_call | solution.py:499
  (16 shorter events, 0.6 us)
Async XLA Ops:
  1.6 4.3 %collective-permute-start = (f32[144,128]{1,0:T(8,128)S(1)}, f32[144,128]{1,0:T(8,128)S(1)}, u32[]{:S(2)}, u32[]{:S(2)}) collective-permute-start(f32[144,128]{1,0:T(8,128)S(1)} %get-tuple-element.38), channel_id=1, source_target_pairs={{0,8},{16,24},{8,0},{24,16},{1,9},{17,25},{9,1},{25,17},{2,10},{18... | collective-permute-start | bytes 221192 | tf_op jit(solution)/shard_map/ppermute | solution.py:532
  2.2 3.8 %collective-permute-start.1 = (f32[144,128]{1,0:T(8,128)S(1)}, f32[144,128]{1,0:T(8,128)S(1)}, u32[]{:S(2)}, u32[]{:S(2)}) collective-permute-start(f32[144,128]{1,0:T(8,128)S(1)} %get-tuple-element.39), channel_id=1, source_target_pairs={{8,16},{16,8},{9,17},{17,9},{10,18},{18,10},{11,19},{19,11},{12,20... | collective-permute-start | bytes 221192 | tf_op jit(solution)/shard_map/ppermute | solution.py:532
  6.3 9.5 %collective-permute-start.2 = (f32[144,128]{1,0:T(8,128)S(1)}, f32[144,128]{1,0:T(8,128)S(1)}, u32[]{:S(2)}, u32[]{:S(2)}) collective-permute-start(f32[144,128]{1,0:T(8,128)S(1)} %get-tuple-element.41), channel_id=1, source_target_pairs={{0,4},{1,5},{2,6},{3,7},{4,0},{5,1},{6,2},{7,3},{8,12},{9,13},{10,... | collective-permute-start | bytes 221192 | tf_op jit(solution)/shard_map/ppermute | solution.py:542
  9.9 7.5 %collective-permute-start.3 = (f32[144,128]{1,0:T(8,128)S(1)}, f32[144,128]{1,0:T(8,128)S(1)}, u32[]{:S(2)}, u32[]{:S(2)}) collective-permute-start(f32[144,128]{1,0:T(8,128)S(1)} %get-tuple-element.42), channel_id=1, source_target_pairs={{0,1},{1,0},{2,3},{3,2},{4,5},{5,4},{6,7},{7,6},{8,9},{9,8},{10,11... | collective-permute-start | bytes 221192 | tf_op jit(solution)/shard_map/ppermute | solution.py:542
  11.4 6.8 %collective-permute-start.4 = (f32[144,128]{1,0:T(8,128)S(1)}, f32[144,128]{1,0:T(8,128)S(1)}, u32[]{:S(2)}, u32[]{:S(2)}) collective-permute-start(f32[144,128]{1,0:T(8,128)S(1)} %get-tuple-element.43), channel_id=1, source_target_pairs={{0,6},{1,7},{2,4},{3,5},{4,2},{5,3},{6,0},{7,1},{8,14},{9,15},{10,... | collective-permute-start | bytes 221192 | tf_op jit(solution)/shard_map/ppermute | solution.py:542
  12.8 6.3 %collective-permute-start.5 = (f32[144,128]{1,0:T(8,128)S(1)}, f32[144,128]{1,0:T(8,128)S(1)}, u32[]{:S(2)}, u32[]{:S(2)}) collective-permute-start(f32[144,128]{1,0:T(8,128)S(1)} %get-tuple-element.44), channel_id=1, source_target_pairs={{0,2},{1,3},{2,0},{3,1},{4,6},{5,7},{6,4},{7,5},{8,10},{9,11},{10,... | collective-permute-start | bytes 221192 | tf_op jit(solution)/shard_map/ppermute | solution.py:542
  13.0 9.5 %collective-permute-start.6 = (f32[144,128]{1,0:T(8,128)S(1)}, f32[144,128]{1,0:T(8,128)S(1)}, u32[]{:S(2)}, u32[]{:S(2)}) collective-permute-start(f32[144,128]{1,0:T(8,128)S(1)} %get-tuple-element.46), channel_id=1, source_target_pairs={{0,5},{1,4},{2,7},{3,6},{4,1},{5,0},{6,3},{7,2},{8,13},{9,12},{10,... | collective-permute-start | bytes 221192 | tf_op jit(solution)/shard_map/ppermute | solution.py:542
  15.8 6.8 %collective-permute-start.7 = (f32[144,128]{1,0:T(8,128)S(1)}, f32[144,128]{1,0:T(8,128)S(1)}, u32[]{:S(2)}, u32[]{:S(2)}) collective-permute-start(f32[144,128]{1,0:T(8,128)S(1)} %get-tuple-element.47), channel_id=1, source_target_pairs={{0,3},{1,2},{2,1},{3,0},{4,7},{5,6},{6,5},{7,4},{8,11},{9,10},{10,... | collective-permute-start | bytes 221192 | tf_op jit(solution)/shard_map/ppermute | solution.py:542
  17.4 7.7 %collective-permute-start.8 = (f32[144,128]{1,0:T(8,128)S(1)}, f32[144,128]{1,0:T(8,128)S(1)}, u32[]{:S(2)}, u32[]{:S(2)}) collective-permute-start(f32[144,128]{1,0:T(8,128)S(1)} %get-tuple-element.50), channel_id=1, source_target_pairs={{0,7},{1,6},{2,5},{3,4},{4,3},{5,2},{6,1},{7,0},{8,15},{9,14},{10,... | collective-permute-start | bytes 221192 | tf_op jit(solution)/shard_map/ppermute | solution.py:542
  27.5 6.1 %collective-permute-start.9 = (f32[16,1152]{1,0:T(8,128)S(1)}, f32[16,1152]{1,0:T(8,128)S(1)}, u32[]{:S(2)}, u32[]{:S(2)}) collective-permute-start(f32[16,1152]{1,0:T(8,128)S(1)} %get-tuple-element.52), channel_id=1, source_target_pairs={{0,8},{16,24},{8,0},{24,16},{1,9},{17,25},{9,1},{25,17},{2,10},{18... | collective-permute-start | bytes 221192 | tf_op jit(solution)/shard_map/ppermute | solution.py:532
  27.9 5.7 %collective-permute-start.10 = (f32[16,1152]{1,0:T(8,128)S(1)}, f32[16,1152]{1,0:T(8,128)S(1)}, u32[]{:S(2)}, u32[]{:S(2)}) collective-permute-start(f32[16,1152]{1,0:T(8,128)S(1)} %get-tuple-element.53), channel_id=1, source_target_pairs={{8,16},{16,8},{9,17},{17,9},{10,18},{18,10},{11,19},{19,11},{12,20... | collective-permute-start | bytes 221192 | tf_op jit(solution)/shard_map/ppermute | solution.py:532
  28.6 4.0 %collective-permute-start.11 = (f32[8,1152]{1,0:T(8,128)S(1)}, f32[8,1152]{1,0:T(8,128)S(1)}, u32[]{:S(2)}, u32[]{:S(2)}) collective-permute-start(f32[8,1152]{1,0:T(8,128)S(1)} %get-tuple-element.54), channel_id=1, source_target_pairs={{0,2},{4,6},{7,5},{3,1},{2,0},{6,4},{5,7},{1,3},{8,10},{12,14},{15... | collective-permute-start | bytes 110600 | tf_op jit(solution)/shard_map/ppermute | solution.py:538
  29.6 4.0 %collective-permute-start.12 = (f32[8,1152]{1,0:T(8,128)S(1)}, f32[8,1152]{1,0:T(8,128)S(1)}, u32[]{:S(2)}, u32[]{:S(2)}) collective-permute-start(f32[8,1152]{1,0:T(8,128)S(1)} %get-tuple-element.55), channel_id=1, source_target_pairs={{2,4},{6,7},{5,3},{1,0},{4,2},{7,6},{3,5},{0,1},{10,12},{14,15},{1... | collective-permute-start | bytes 110600 | tf_op jit(solution)/shard_map/ppermute | solution.py:538
  36.3 9.1 %collective-permute-start.13 = (f32[144,128]{1,0:T(8,128)S(1)}, f32[144,128]{1,0:T(8,128)S(1)}, u32[]{:S(2)}, u32[]{:S(2)}) collective-permute-start(f32[144,128]{1,0:T(8,128)S(1)} %get-tuple-element.58), channel_id=1, source_target_pairs={{0,4},{1,5},{2,6},{3,7},{4,0},{5,1},{6,2},{7,3},{8,12},{9,13},{10,... | collective-permute-start | bytes 221192 | tf_op jit(solution)/shard_map/ppermute | solution.py:542
  39.5 5.9 %collective-permute-start.14 = (f32[144,128]{1,0:T(8,128)S(1)}, f32[144,128]{1,0:T(8,128)S(1)}, u32[]{:S(2)}, u32[]{:S(2)}) collective-permute-start(f32[144,128]{1,0:T(8,128)S(1)} %get-tuple-element.59), channel_id=1, source_target_pairs={{0,1},{1,0},{2,3},{3,2},{4,5},{5,4},{6,7},{7,6},{8,9},{9,8},{10,11... | collective-permute-start | bytes 221192 | tf_op jit(solution)/shard_map/ppermute | solution.py:542
  39.5 7.9 %collective-permute-start.15 = (f32[144,128]{1,0:T(8,128)S(1)}, f32[144,128]{1,0:T(8,128)S(1)}, u32[]{:S(2)}, u32[]{:S(2)}) collective-permute-start(f32[144,128]{1,0:T(8,128)S(1)} %get-tuple-element.60), channel_id=1, source_target_pairs={{0,6},{1,7},{2,4},{3,5},{4,2},{5,3},{6,0},{7,1},{8,14},{9,15},{10,... | collective-permute-start | bytes 221192 | tf_op jit(solution)/shard_map/ppermute | solution.py:542
  40.4 7.0 %collective-permute-start.16 = (f32[144,128]{1,0:T(8,128)S(1)}, f32[144,128]{1,0:T(8,128)S(1)}, u32[]{:S(2)}, u32[]{:S(2)}) collective-permute-start(f32[144,128]{1,0:T(8,128)S(1)} %get-tuple-element.61), channel_id=1, source_target_pairs={{0,2},{1,3},{2,0},{3,1},{4,6},{5,7},{6,4},{7,5},{8,10},{9,11},{10,... | collective-permute-start | bytes 221192 | tf_op jit(solution)/shard_map/ppermute | solution.py:542
  40.9 8.8 %collective-permute-start.17 = (f32[144,128]{1,0:T(8,128)S(1)}, f32[144,128]{1,0:T(8,128)S(1)}, u32[]{:S(2)}, u32[]{:S(2)}) collective-permute-start(f32[144,128]{1,0:T(8,128)S(1)} %get-tuple-element.62), channel_id=1, source_target_pairs={{0,5},{1,4},{2,7},{3,6},{4,1},{5,0},{6,3},{7,2},{8,13},{9,12},{10,... | collective-permute-start | bytes 221192 | tf_op jit(solution)/shard_map/ppermute | solution.py:542
  45.4 6.3 %collective-permute-start.18 = (f32[144,128]{1,0:T(8,128)S(1)}, f32[144,128]{1,0:T(8,128)S(1)}, u32[]{:S(2)}, u32[]{:S(2)}) collective-permute-start(f32[144,128]{1,0:T(8,128)S(1)} %get-tuple-element.63), channel_id=1, source_target_pairs={{0,3},{1,2},{2,1},{3,0},{4,7},{5,6},{6,5},{7,4},{8,11},{9,10},{10,... | collective-permute-start | bytes 221192 | tf_op jit(solution)/shard_map/ppermute | solution.py:542
  45.4 8.8 %collective-permute-start.19 = (f32[144,128]{1,0:T(8,128)S(1)}, f32[144,128]{1,0:T(8,128)S(1)}, u32[]{:S(2)}, u32[]{:S(2)}) collective-permute-start(f32[144,128]{1,0:T(8,128)S(1)} %get-tuple-element.64), channel_id=1, source_target_pairs={{0,7},{1,6},{2,5},{3,4},{4,3},{5,2},{6,1},{7,0},{8,15},{9,14},{10,... | collective-permute-start | bytes 221192 | tf_op jit(solution)/shard_map/ppermute | solution.py:542
where the time goes:
time: 56.6 us; the launch traced here: 56.4 us
  starting transfers between devices  27.3 us (48%)
  Pallas kernels  15.3 us (27%)
  waiting for transfers between devices  13.7 us (24%)
    ppermute x14, starting transfers between devices, swap_blocks(): lax.ppermute(block, 'wide', [(w, w ^ k) for w in range(wide)])  23 us
    pallas_call x8, Pallas kernels, on_chip(): made(*(pltpu.with_memory_space_constraint(one, spec.memory_space) for one...  15.3 us
    ppermute x14, waiting for transfers between devices, swap_blocks(): lax.ppermute(block, 'wide', [(w, w ^ k) for w in range(wide)])  10.7 us
    ppermute x1, waiting for transfers between devices, swap_cols(): lax.ppermute(c, 'wide', along(0))  2.06 us
    ppermute x2, starting transfers between devices, swap_rows(): lax.ppermute(b, 'slab', pairs(slabs, 1))  1.31 us
  transfers between devices with their start and end apart: 20, of which 8 were waited for; matrix products, arithmetic and copies ran while one was open for 0% of the time, Pallas kernels for 11%

commit v1 on v0

--- a/solution.py
+++ b/solution.py
@@ -147,7 +147,11 @@
             if a & bit:
                 continue
             b = a | bit
-            crossed = jnp.take_along_axis(jnp.where(low, parts[b], parts[a]), other, axis=1)
+            crossed = jnp.where(low, parts[b], parts[a])
+            if 2 * bit * width == LANES:
+                crossed = pltpu.roll(crossed, bit * width, 1)
+            else:
+                crossed = jnp.take_along_axis(crossed, other, axis=1)
             done[a] = jnp.where(low, parts[a], crossed)
             done[b] = jnp.where(low, crossed, parts[b])
         parts = done

time: 56.6 us -> 56.5 us (level)
  no operation moved by 1% of the time
where the time goes in v1:
time: 56.5 us; the launch traced here: 56.3 us
  starting transfers between devices  27.4 us (48%)
  Pallas kernels  15 us (27%)
  waiting for transfers between devices  13.8 us (24%)
    ppermute x14, starting transfers between devices, swap_blocks(): lax.ppermute(block, 'wide', [(w, w ^ k) for w in range(wide)])  23.1 us
    pallas_call x8, Pallas kernels, on_chip(): made(*(pltpu.with_memory_space_constraint(one, spec.memory_space) for one...  15 us
    ppermute x14, waiting for transfers between devices, swap_blocks(): lax.ppermute(block, 'wide', [(w, w ^ k) for w in range(wide)])  10.8 us
    ppermute x1, waiting for transfers between devices, swap_cols(): lax.ppermute(c, 'wide', along(0))  2.05 us
    ppermute x2, starting transfers between devices, swap_rows(): lax.ppermute(b, 'slab', pairs(slabs, 1))  1.31 us
  transfers between devices with their start and end apart: 20, of which 8 were waited for; matrix products, arithmetic and copies ran while one was open for 0% of the time, Pallas kernels for 11%

profile of v1, /device:TPU:0, one launch (start us, length us, event | category | flops | bytes accessed | tf_op | source)
XLA Modules:
  0.0 56.3 jit_solution(7960557152835842993)
XLA Ops:
  0.0 1.6 %shard_map.64 = (f32[144,128]{1,0:T(8,128)S(1)}, f32[144,128]{1,0:T(8,128)S(1)}, f32[8,152,128]{2,1,0:T(8,128)S(1)}, f32[8,128]{1,0:T(8,128)S(1)}, f32[5,152,128]{2,1,0:T(8,128)S(1)}) custom-call(f32[144,8,128]{2,1,0:T(8,128)} %x_hbm.1, s32[8,128]{1,0:T(8,128)} %mask_hbm.1, s32[9,128]{1,0:T(8,128)} %bitcast.2, f32[1,32]{1,0:T(1,128)} %bitcast.3, ...), custom_call_target="tpu_custom_call" | custom-call | tf_op jit(solution)/shard_map/pallas_call | solution.py:503
  1.6 0.6 collective-permute-start
  2.2 0.7 %collective-permute-start.1 = (f32[144,128]{1,0:T(8,128)S(1)}, f32[144,128]{1,0:T(8,128)S(1)}, u32[]{:S(2)}, u32[]{:S(2)}) collective-permute-start(f32[144,128]{1,0:T(8,128)S(1)} %get-tuple-element.39), channel_id=1, source_target_pairs={{8,16},{16,8},{9,17},{17,9},{10,18},{18,10},{11,19},{19,11},{12,20... | collective-permute-start | bytes 221192 | tf_op jit(solution)/shard_map/ppermute | solution.py:536
  2.8 3.3 %shard_map.65.x_ref = f32[8,152,128]{2,1,0:T(8,128)S(1)} custom-call(f32[8,152,128]{2,1,0:T(8,128)S(1)} %get-tuple-element.36.x_ref, f32[8,128]{1,0:T(8,128)S(1)} %get-tuple-element.35.sea_ref, f32[5,152,128]{2,1,0:T(8,128)S(1)} %get-tuple-element.37.own_ref), custom_call_target="tpu_custom_call" | custom-call | flops 1000000000 | tf_op jit(solution)/shard_map/pallas_call | solution.py:503
  6.4 3.7 %collective-permute-start.2 = (f32[144,128]{1,0:T(8,128)S(1)}, f32[144,128]{1,0:T(8,128)S(1)}, u32[]{:S(2)}, u32[]{:S(2)}) collective-permute-start(f32[144,128]{1,0:T(8,128)S(1)} %get-tuple-element.41), channel_id=1, source_target_pairs={{0,4},{1,5},{2,6},{3,7},{4,0},{5,1},{6,2},{7,3},{8,12},{9,13},{10,... | collective-permute-start | bytes 221192 | tf_op jit(solution)/shard_map/ppermute | solution.py:546
  10.1 1.5 %collective-permute-start.3 = (f32[144,128]{1,0:T(8,128)S(1)}, f32[144,128]{1,0:T(8,128)S(1)}, u32[]{:S(2)}, u32[]{:S(2)}) collective-permute-start(f32[144,128]{1,0:T(8,128)S(1)} %get-tuple-element.42), channel_id=1, source_target_pairs={{0,1},{1,0},{2,3},{3,2},{4,5},{5,4},{6,7},{7,6},{8,9},{9,8},{10,11... | collective-permute-start | bytes 221192 | tf_op jit(solution)/shard_map/ppermute | solution.py:546
  11.6 1.3 %collective-permute-start.4 = (f32[144,128]{1,0:T(8,128)S(1)}, f32[144,128]{1,0:T(8,128)S(1)}, u32[]{:S(2)}, u32[]{:S(2)}) collective-permute-start(f32[144,128]{1,0:T(8,128)S(1)} %get-tuple-element.43), channel_id=1, source_target_pairs={{0,6},{1,7},{2,4},{3,5},{4,2},{5,3},{6,0},{7,1},{8,14},{9,15},{10,... | collective-permute-start | bytes 221192 | tf_op jit(solution)/shard_map/ppermute | solution.py:546
  13.2 2.8 %collective-permute-start.6 = (f32[144,128]{1,0:T(8,128)S(1)}, f32[144,128]{1,0:T(8,128)S(1)}, u32[]{:S(2)}, u32[]{:S(2)}) collective-permute-start(f32[144,128]{1,0:T(8,128)S(1)} %get-tuple-element.46), channel_id=1, source_target_pairs={{0,5},{1,4},{2,7},{3,6},{4,1},{5,0},{6,3},{7,2},{8,13},{9,12},{10,... | collective-permute-start | bytes 221192 | tf_op jit(solution)/shard_map/ppermute | solution.py:546
  16.0 1.6 %collective-permute-start.7 = (f32[144,128]{1,0:T(8,128)S(1)}, f32[144,128]{1,0:T(8,128)S(1)}, u32[]{:S(2)}, u32[]{:S(2)}) collective-permute-start(f32[144,128]{1,0:T(8,128)S(1)} %get-tuple-element.47), channel_id=1, source_target_pairs={{0,3},{1,2},{2,1},{3,0},{4,7},{5,6},{6,5},{7,4},{8,11},{9,10},{10,... | collective-permute-start | bytes 221192 | tf_op jit(solution)/shard_map/ppermute | solution.py:546
  17.6 0.9 %collective-permute-start.8 = (f32[144,128]{1,0:T(8,128)S(1)}, f32[144,128]{1,0:T(8,128)S(1)}, u32[]{:S(2)}, u32[]{:S(2)}) collective-permute-start(f32[144,128]{1,0:T(8,128)S(1)} %get-tuple-element.50), channel_id=1, source_target_pairs={{0,7},{1,6},{2,5},{3,4},{4,3},{5,2},{6,1},{7,0},{8,15},{9,14},{10,... | collective-permute-start | bytes 221192 | tf_op jit(solution)/shard_map/ppermute | solution.py:546
  18.4 0.8 %collective-permute-done.5.refs_4_ = f32[144,128]{1,0:T(8,128)S(1)} collective-permute-done((f32[144,128]{1,0:T(8,128)S(1)}, f32[144,128]{1,0:T(8,128)S(1)}, u32[]{:S(2)}, u32[]{:S(2)}) %collective-permute-start.5) | collective-permute-done | bytes 73760 | tf_op jit(solution)/shard_map/ppermute | solution.py:546
  19.2 1.9 %shard_map.67 = (f32[1152,128]{1,0:T(8,128)S(1)}, f32[128,128]{1,0:T(8,128)S(1)}, bf16[1152,1152]{1,0:T(8,128)(2,1)S(1)}, f32[8,1152]{1,0:T(8,128)S(1)}) custom-call(s32[1152]{0:T(1024)} %owner_ref.3, f32[1,32]{1,0:T(1,128)} %bitcast.4, f32[2,128]{1,0:T(2,128)} %constant.2.clone.table_hbm, bf16[1152,1152]{1,0:T(8,128)(2,1)} %coupling_hbm.1, ...), custom_call_target="tpu_custom_call" | custom-call | flops 1000000000 | tf_op jit(solution)/shard_map/pallas_call | solution.py:503
  21.1 1.6 %collective-permute-done.6.refs_0_ = f32[144,128]{1,0:T(8,128)S(1)} collective-permute-done((f32[144,128]{1,0:T(8,128)S(1)}, f32[144,128]{1,0:T(8,128)S(1)}, u32[]{:S(2)}, u32[]{:S(2)}) %collective-permute-start.6) | collective-permute-done | bytes 73760 | tf_op jit(solution)/shard_map/ppermute | solution.py:546
  22.7 1.1 %shard_map.68.held_ref = f32[1152,128]{1,0:T(8,128)S(1)} custom-call(f32[1152,128]{1,0:T(8,128)S(1)} %get-tuple-element.45.held_ref, s32[1152]{0:T(1024)} %owner_ref.3, f32[144,128]{1,0:T(8,128)S(1)} %collective-permute-done.6.refs_0_, f32[144,128]{1,0:T(8,128)S(1)} %collective-permute-done.7.refs_1_), custom_call_target="tpu_custom_call", output_to_operand_aliasing={{}: (0, {})} | custom-call | flops 1000000000 | tf_op jit(solution)/shard_map/pallas_call | solution.py:503
  23.8 1.5 %collective-permute-done.8.refs_0_ = f32[144,128]{1,0:T(8,128)S(1)} collective-permute-done((f32[144,128]{1,0:T(8,128)S(1)}, f32[144,128]{1,0:T(8,128)S(1)}, u32[]{:S(2)}, u32[]{:S(2)}) %collective-permute-start.8) | collective-permute-done | bytes 73760 | tf_op jit(solution)/shard_map/ppermute | solution.py:546
  25.3 2.4 %shard_map.69 = (f32[1152,128]{1,0:T(8,128)S(1)}, f32[128,1152]{1,0:T(8,128)S(1)}, f32[16,1152]{1,0:T(8,128)S(1)}, f32[16,1152]{1,0:T(8,128)S(1)}, f32[8,1152]{1,0:T(8,128)S(1)}, /*index=5*/f32[8,1152]{1,0:T(8,128)S(1)}) custom-call(f32[1152,128]{1,0:T(8,128)S(1)} %shard_map.68.held_ref, s32[1152]{0:T(1024)} %owner_ref.3, ...), custom_call_target="tpu_custom_call", output_to_operand_aliasing={{0}: (0, {})} | custom-call | flops 679477248 | tf_op jit(solution)/shard_map/pallas_call | solution.py:503
  27.7 0.4 collective-permute-start.9
  28.1 0.7 %collective-permute-start.10 = (f32[16,1152]{1,0:T(8,128)S(1)}, f32[16,1152]{1,0:T(8,128)S(1)}, u32[]{:S(2)}, u32[]{:S(2)}) collective-permute-start(f32[16,1152]{1,0:T(8,128)S(1)} %get-tuple-element.53), channel_id=1, source_target_pairs={{8,16},{16,8},{9,17},{17,9},{10,18},{18,10},{11,19},{19,11},{12,20... | collective-permute-start | bytes 221192 | tf_op jit(solution)/shard_map/ppermute | solution.py:536
  28.8 1.0 %collective-permute-start.11 = (f32[8,1152]{1,0:T(8,128)S(1)}, f32[8,1152]{1,0:T(8,128)S(1)}, u32[]{:S(2)}, u32[]{:S(2)}) collective-permute-start(f32[8,1152]{1,0:T(8,128)S(1)} %get-tuple-element.54), channel_id=1, source_target_pairs={{0,2},{4,6},{7,5},{3,1},{2,0},{6,4},{5,7},{1,3},{8,10},{12,14},{15... | collective-permute-start | bytes 110600 | tf_op jit(solution)/shard_map/ppermute | solution.py:542
  29.8 0.9 %collective-permute-start.12 = (f32[8,1152]{1,0:T(8,128)S(1)}, f32[8,1152]{1,0:T(8,128)S(1)}, u32[]{:S(2)}, u32[]{:S(2)}) collective-permute-start(f32[8,1152]{1,0:T(8,128)S(1)} %get-tuple-element.55), channel_id=1, source_target_pairs={{2,4},{6,7},{5,3},{1,0},{4,2},{7,6},{3,5},{0,1},{10,12},{14,15},{1... | collective-permute-start | bytes 110600 | tf_op jit(solution)/shard_map/ppermute | solution.py:542
  30.7 2.1 %collective-permute-done.11.c_ref = f32[8,1152]{1,0:T(8,128)S(1)} collective-permute-done((f32[8,1152]{1,0:T(8,128)S(1)}, f32[8,1152]{1,0:T(8,128)S(1)}, u32[]{:S(2)}, u32[]{:S(2)}) %collective-permute-start.11) | collective-permute-done | bytes 36896 | tf_op jit(solution)/shard_map/ppermute | solution.py:542
  32.8 1.0 %collective-permute-done.12.d_ref = f32[8,1152]{1,0:T(8,128)S(1)} collective-permute-done((f32[8,1152]{1,0:T(8,128)S(1)}, f32[8,1152]{1,0:T(8,128)S(1)}, u32[]{:S(2)}, u32[]{:S(2)}) %collective-permute-start.12) | collective-permute-done | bytes 36896 | tf_op jit(solution)/shard_map/ppermute | solution.py:542
  33.7 2.7 %shard_map.70 = (f32[144,128]{1,0:T(8,128)S(1)}, f32[144,128]{1,0:T(8,128)S(1)}, f32[144,128]{1,0:T(8,128)S(1)}, f32[144,128]{1,0:T(8,128)S(1)}, f32[144,128]{1,...) custom-call(f32[128,1152]{1,0:T(8,128)S(1)} %get-tuple-element.51.x_ref, ...), custom_call_target="tpu_custom_call" | custom-call | flops 679477248 | tf_op jit(solution)/shard_map/pallas_call | solution.py:503
  36.5 3.2 %collective-permute-start.13 = (f32[144,128]{1,0:T(8,128)S(1)}, f32[144,128]{1,0:T(8,128)S(1)}, u32[]{:S(2)}, u32[]{:S(2)}) collective-permute-start(f32[144,128]{1,0:T(8,128)S(1)} %get-tuple-element.58), channel_id=1, source_target_pairs={{0,4},{1,5},{2,6},{3,7},{4,0},{5,1},{6,2},{7,3},{8,12},{9,13},{10,... | collective-permute-start | bytes 221192 | tf_op jit(solution)/shard_map/ppermute | solution.py:546
  39.7 0.9 %collective-permute-start.15 = (f32[144,128]{1,0:T(8,128)S(1)}, f32[144,128]{1,0:T(8,128)S(1)}, u32[]{:S(2)}, u32[]{:S(2)}) collective-permute-start(f32[144,128]{1,0:T(8,128)S(1)} %get-tuple-element.60), channel_id=1, source_target_pairs={{0,6},{1,7},{2,4},{3,5},{4,2},{5,3},{6,0},{7,1},{8,14},{9,15},{10,... | collective-permute-start | bytes 221192 | tf_op jit(solution)/shard_map/ppermute | solution.py:546
  40.6 0.5 collective-permute-start.16
  41.1 4.5 %collective-permute-start.17 = (f32[144,128]{1,0:T(8,128)S(1)}, f32[144,128]{1,0:T(8,128)S(1)}, u32[]{:S(2)}, u32[]{:S(2)}) collective-permute-start(f32[144,128]{1,0:T(8,128)S(1)} %get-tuple-element.62), channel_id=1, source_target_pairs={{0,5},{1,4},{2,7},{3,6},{4,1},{5,0},{6,3},{7,2},{8,13},{9,12},{10,... | collective-permute-start | bytes 221192 | tf_op jit(solution)/shard_map/ppermute | solution.py:546
  45.6 2.1 %collective-permute-start.19 = (f32[144,128]{1,0:T(8,128)S(1)}, f32[144,128]{1,0:T(8,128)S(1)}, u32[]{:S(2)}, u32[]{:S(2)}) collective-permute-start(f32[144,128]{1,0:T(8,128)S(1)} %get-tuple-element.64), channel_id=1, source_target_pairs={{0,7},{1,6},{2,5},{3,4},{4,3},{5,2},{6,1},{7,0},{8,15},{9,14},{10,... | collective-permute-start | bytes 221192 | tf_op jit(solution)/shard_map/ppermute | solution.py:546
  47.6 2.1 %collective-permute-done.17.refs_5_ = f32[144,128]{1,0:T(8,128)S(1)} collective-permute-done((f32[144,128]{1,0:T(8,128)S(1)}, f32[144,128]{1,0:T(8,128)S(1)}, u32[]{:S(2)}, u32[]{:S(2)}) %collective-permute-start.17) | collective-permute-done | bytes 73760 | tf_op jit(solution)/shard_map/ppermute | solution.py:546
  49.8 2.2 %collective-permute-done.18.refs_6_ = f32[144,128]{1,0:T(8,128)S(1)} collective-permute-done((f32[144,128]{1,0:T(8,128)S(1)}, f32[144,128]{1,0:T(8,128)S(1)}, u32[]{:S(2)}, u32[]{:S(2)}) %collective-permute-start.18) | collective-permute-done | bytes 73760 | tf_op jit(solution)/shard_map/ppermute | solution.py:546
  51.9 2.6 %collective-permute-done.19.refs_7_ = f32[144,128]{1,0:T(8,128)S(1)} collective-permute-done((f32[144,128]{1,0:T(8,128)S(1)}, f32[144,128]{1,0:T(8,128)S(1)}, u32[]{:S(2)}, u32[]{:S(2)}) %collective-permute-start.19) | collective-permute-done | bytes 73760 | tf_op jit(solution)/shard_map/ppermute | solution.py:546
  54.5 1.8 %shard_map.71 = f32[144,8,128]{2,1,0:T(8,128)} custom-call(f32[144,128]{1,0:T(8,128)S(1)} %get-tuple-element.57.refs_0_, f32[144,128]{1,0:T(8,128)S(1)} %collective-permute-done.13.refs_1_, f32[144,128]{1,0:T(8,128)S(1)} %collective-permute-done.14.refs_2_, f32[144,128]{1,0:T(8,128)S(1)} %collective-permute-done.15.refs_3_, ...), custom_call_target="tpu_custom_call" | custom-call | tf_op jit(solution)/shard_map/pallas_call | solution.py:503
  (16 shorter events, 0.6 us)
Async XLA Ops:
  1.6 4.5 %collective-permute-start = (f32[144,128]{1,0:T(8,128)S(1)}, f32[144,128]{1,0:T(8,128)S(1)}, u32[]{:S(2)}, u32[]{:S(2)}) collective-permute-start(f32[144,128]{1,0:T(8,128)S(1)} %get-tuple-element.38), channel_id=1, source_target_pairs={{0,8},{16,24},{8,0},{24,16},{1,9},{17,25},{9,1},{25,17},{2,10},{18... | collective-permute-start | bytes 221192 | tf_op jit(solution)/shard_map/ppermute | solution.py:536
  2.2 3.9 %collective-permute-start.1 = (f32[144,128]{1,0:T(8,128)S(1)}, f32[144,128]{1,0:T(8,128)S(1)}, u32[]{:S(2)}, u32[]{:S(2)}) collective-permute-start(f32[144,128]{1,0:T(8,128)S(1)} %get-tuple-element.39), channel_id=1, source_target_pairs={{8,16},{16,8},{9,17},{17,9},{10,18},{18,10},{11,19},{19,11},{12,20... | collective-permute-start | bytes 221192 | tf_op jit(solution)/shard_map/ppermute | solution.py:536
  6.4 9.5 %collective-permute-start.2 = (f32[144,128]{1,0:T(8,128)S(1)}, f32[144,128]{1,0:T(8,128)S(1)}, u32[]{:S(2)}, u32[]{:S(2)}) collective-permute-start(f32[144,128]{1,0:T(8,128)S(1)} %get-tuple-element.41), channel_id=1, source_target_pairs={{0,4},{1,5},{2,6},{3,7},{4,0},{5,1},{6,2},{7,3},{8,12},{9,13},{10,... | collective-permute-start | bytes 221192 | tf_op jit(solution)/shard_map/ppermute | solution.py:546
  10.1 7.5 %collective-permute-start.3 = (f32[144,128]{1,0:T(8,128)S(1)}, f32[144,128]{1,0:T(8,128)S(1)}, u32[]{:S(2)}, u32[]{:S(2)}) collective-permute-start(f32[144,128]{1,0:T(8,128)S(1)} %get-tuple-element.42), channel_id=1, source_target_pairs={{0,1},{1,0},{2,3},{3,2},{4,5},{5,4},{6,7},{7,6},{8,9},{9,8},{10,11... | collective-permute-start | bytes 221192 | tf_op jit(solution)/shard_map/ppermute | solution.py:546
  11.6 6.8 %collective-permute-start.4 = (f32[144,128]{1,0:T(8,128)S(1)}, f32[144,128]{1,0:T(8,128)S(1)}, u32[]{:S(2)}, u32[]{:S(2)}) collective-permute-start(f32[144,128]{1,0:T(8,128)S(1)} %get-tuple-element.43), channel_id=1, source_target_pairs={{0,6},{1,7},{2,4},{3,5},{4,2},{5,3},{6,0},{7,1},{8,14},{9,15},{10,... | collective-permute-start | bytes 221192 | tf_op jit(solution)/shard_map/ppermute | solution.py:546
  12.9 6.3 %collective-permute-start.5 = (f32[144,128]{1,0:T(8,128)S(1)}, f32[144,128]{1,0:T(8,128)S(1)}, u32[]{:S(2)}, u32[]{:S(2)}) collective-permute-start(f32[144,128]{1,0:T(8,128)S(1)} %get-tuple-element.44), channel_id=1, source_target_pairs={{0,2},{1,3},{2,0},{3,1},{4,6},{5,7},{6,4},{7,5},{8,10},{9,11},{10,... | collective-permute-start | bytes 221192 | tf_op jit(solution)/shard_map/ppermute | solution.py:546
  13.2 9.5 %collective-permute-start.6 = (f32[144,128]{1,0:T(8,128)S(1)}, f32[144,128]{1,0:T(8,128)S(1)}, u32[]{:S(2)}, u32[]{:S(2)}) collective-permute-start(f32[144,128]{1,0:T(8,128)S(1)} %get-tuple-element.46), channel_id=1, source_target_pairs={{0,5},{1,4},{2,7},{3,6},{4,1},{5,0},{6,3},{7,2},{8,13},{9,12},{10,... | collective-permute-start | bytes 221192 | tf_op jit(solution)/shard_map/ppermute | solution.py:546
  16.0 6.8 %collective-permute-start.7 = (f32[144,128]{1,0:T(8,128)S(1)}, f32[144,128]{1,0:T(8,128)S(1)}, u32[]{:S(2)}, u32[]{:S(2)}) collective-permute-start(f32[144,128]{1,0:T(8,128)S(1)} %get-tuple-element.47), channel_id=1, source_target_pairs={{0,3},{1,2},{2,1},{3,0},{4,7},{5,6},{6,5},{7,4},{8,11},{9,10},{10,... | collective-permute-start | bytes 221192 | tf_op jit(solution)/shard_map/ppermute | solution.py:546
  17.6 7.7 %collective-permute-start.8 = (f32[144,128]{1,0:T(8,128)S(1)}, f32[144,128]{1,0:T(8,128)S(1)}, u32[]{:S(2)}, u32[]{:S(2)}) collective-permute-start(f32[144,128]{1,0:T(8,128)S(1)} %get-tuple-element.50), channel_id=1, source_target_pairs={{0,7},{1,6},{2,5},{3,4},{4,3},{5,2},{6,1},{7,0},{8,15},{9,14},{10,... | collective-permute-start | bytes 221192 | tf_op jit(solution)/shard_map/ppermute | solution.py:546
  27.7 6.1 %collective-permute-start.9 = (f32[16,1152]{1,0:T(8,128)S(1)}, f32[16,1152]{1,0:T(8,128)S(1)}, u32[]{:S(2)}, u32[]{:S(2)}) collective-permute-start(f32[16,1152]{1,0:T(8,128)S(1)} %get-tuple-element.52), channel_id=1, source_target_pairs={{0,8},{16,24},{8,0},{24,16},{1,9},{17,25},{9,1},{25,17},{2,10},{18... | collective-permute-start | bytes 221192 | tf_op jit(solution)/shard_map/ppermute | solution.py:536
  28.1 5.7 %collective-permute-start.10 = (f32[16,1152]{1,0:T(8,128)S(1)}, f32[16,1152]{1,0:T(8,128)S(1)}, u32[]{:S(2)}, u32[]{:S(2)}) collective-permute-start(f32[16,1152]{1,0:T(8,128)S(1)} %get-tuple-element.53), channel_id=1, source_target_pairs={{8,16},{16,8},{9,17},{17,9},{10,18},{18,10},{11,19},{19,11},{12,20... | collective-permute-start | bytes 221192 | tf_op jit(solution)/shard_map/ppermute | solution.py:536
  28.8 4.0 %collective-permute-start.11 = (f32[8,1152]{1,0:T(8,128)S(1)}, f32[8,1152]{1,0:T(8,128)S(1)}, u32[]{:S(2)}, u32[]{:S(2)}) collective-permute-start(f32[8,1152]{1,0:T(8,128)S(1)} %get-tuple-element.54), channel_id=1, source_target_pairs={{0,2},{4,6},{7,5},{3,1},{2,0},{6,4},{5,7},{1,3},{8,10},{12,14},{15... | collective-permute-start | bytes 110600 | tf_op jit(solution)/shard_map/ppermute | solution.py:542
  29.8 4.0 %collective-permute-start.12 = (f32[8,1152]{1,0:T(8,128)S(1)}, f32[8,1152]{1,0:T(8,128)S(1)}, u32[]{:S(2)}, u32[]{:S(2)}) collective-permute-start(f32[8,1152]{1,0:T(8,128)S(1)} %get-tuple-element.55), channel_id=1, source_target_pairs={{2,4},{6,7},{5,3},{1,0},{4,2},{7,6},{3,5},{0,1},{10,12},{14,15},{1... | collective-permute-start | bytes 110600 | tf_op jit(solution)/shard_map/ppermute | solution.py:542
  36.5 9.1 %collective-permute-start.13 = (f32[144,128]{1,0:T(8,128)S(1)}, f32[144,128]{1,0:T(8,128)S(1)}, u32[]{:S(2)}, u32[]{:S(2)}) collective-permute-start(f32[144,128]{1,0:T(8,128)S(1)} %get-tuple-element.58), channel_id=1, source_target_pairs={{0,4},{1,5},{2,6},{3,7},{4,0},{5,1},{6,2},{7,3},{8,12},{9,13},{10,... | collective-permute-start | bytes 221192 | tf_op jit(solution)/shard_map/ppermute | solution.py:546
  39.7 5.9 %collective-permute-start.14 = (f32[144,128]{1,0:T(8,128)S(1)}, f32[144,128]{1,0:T(8,128)S(1)}, u32[]{:S(2)}, u32[]{:S(2)}) collective-permute-start(f32[144,128]{1,0:T(8,128)S(1)} %get-tuple-element.59), channel_id=1, source_target_pairs={{0,1},{1,0},{2,3},{3,2},{4,5},{5,4},{6,7},{7,6},{8,9},{9,8},{10,11... | collective-permute-start | bytes 221192 | tf_op jit(solution)/shard_map/ppermute | solution.py:546
  39.7 8.0 %collective-permute-start.15 = (f32[144,128]{1,0:T(8,128)S(1)}, f32[144,128]{1,0:T(8,128)S(1)}, u32[]{:S(2)}, u32[]{:S(2)}) collective-permute-start(f32[144,128]{1,0:T(8,128)S(1)} %get-tuple-element.60), channel_id=1, source_target_pairs={{0,6},{1,7},{2,4},{3,5},{4,2},{5,3},{6,0},{7,1},{8,14},{9,15},{10,... | collective-permute-start | bytes 221192 | tf_op jit(solution)/shard_map/ppermute | solution.py:546
  40.6 7.1 %collective-permute-start.16 = (f32[144,128]{1,0:T(8,128)S(1)}, f32[144,128]{1,0:T(8,128)S(1)}, u32[]{:S(2)}, u32[]{:S(2)}) collective-permute-start(f32[144,128]{1,0:T(8,128)S(1)} %get-tuple-element.61), channel_id=1, source_target_pairs={{0,2},{1,3},{2,0},{3,1},{4,6},{5,7},{6,4},{7,5},{8,10},{9,11},{10,... | collective-permute-start | bytes 221192 | tf_op jit(solution)/shard_map/ppermute | solution.py:546
  41.1 8.7 %collective-permute-start.17 = (f32[144,128]{1,0:T(8,128)S(1)}, f32[144,128]{1,0:T(8,128)S(1)}, u32[]{:S(2)}, u32[]{:S(2)}) collective-permute-start(f32[144,128]{1,0:T(8,128)S(1)} %get-tuple-element.62), channel_id=1, source_target_pairs={{0,5},{1,4},{2,7},{3,6},{4,1},{5,0},{6,3},{7,2},{8,13},{9,12},{10,... | collective-permute-start | bytes 221192 | tf_op jit(solution)/shard_map/ppermute | solution.py:546
  45.5 6.4 %collective-permute-start.18 = (f32[144,128]{1,0:T(8,128)S(1)}, f32[144,128]{1,0:T(8,128)S(1)}, u32[]{:S(2)}, u32[]{:S(2)}) collective-permute-start(f32[144,128]{1,0:T(8,128)S(1)} %get-tuple-element.63), channel_id=1, source_target_pairs={{0,3},{1,2},{2,1},{3,0},{4,7},{5,6},{6,5},{7,4},{8,11},{9,10},{10,... | collective-permute-start | bytes 221192 | tf_op jit(solution)/shard_map/ppermute | solution.py:546
  45.6 9.0 %collective-permute-start.19 = (f32[144,128]{1,0:T(8,128)S(1)}, f32[144,128]{1,0:T(8,128)S(1)}, u32[]{:S(2)}, u32[]{:S(2)}) collective-permute-start(f32[144,128]{1,0:T(8,128)S(1)} %get-tuple-element.64), channel_id=1, source_target_pairs={{0,7},{1,6},{2,5},{3,4},{4,3},{5,2},{6,1},{7,0},{8,15},{9,14},{10,... | collective-permute-start | bytes 221192 | tf_op jit(solution)/shard_map/ppermute | solution.py:546
